TPU v7x, 32 devices: a whole 2x2x4 slice. The times are simulated.
32 devices in a mesh: rep: 2 (over x), exp: 4 (over z), ten: 4 (over y, core).
Axes of the slice: x: 2, y: 2, z: 4, core: 2. Of those that a mesh axis runs over, the one named last changes fastest.
Arguments:
- hidden_in: bfloat16 [768, 3072], P(('rep', 'exp', 'ten')), parts along dimension 0, may hold values from -6 to 6
- queries: bfloat16 [768, 6144], P(('rep', 'exp', 'ten')), parts along dimension 0, may hold values from -100 to 100
- new_kv: bfloat16 [2, 768, 1024], P(None, ('rep', 'exp', 'ten')), parts along dimension 1, may hold values from -5 to 5
- prefix_kv: bfloat16 [2, 8, 128, 1024], P(None, ('rep', 'exp'), 'ten'), parts along dimension 1, may hold values from -5 to 5
- decode_kv: bfloat16 [2, 128, 48, 1024], P(None, ('rep', 'exp', 'ten')), parts along dimension 1, may hold values from -5 to 5
- prefix_len: int32 [8], P(('rep', 'exp')), parts along dimension 0, may hold values from 2 to 128
- decode_len: int32 [128], P(('rep', 'exp', 'ten')), parts along dimension 0, may hold values from 2 to 48
- out_proj: bfloat16 [6144, 3072], P('ten'), may hold values from -0.078125 to 0.078125
- norm_gain: float32 [3072], replicated, may hold values from 0.5 to 1.5
- router_w: bfloat16 [3072, 8], replicated, may hold values from -0.109375 to 0.109375
- expert_ids: int32 [768, 2], P(('rep', 'exp', 'ten')), parts along dimension 0, may hold values from 0 to 7, all different within a row; in each aligned block of 24 rows (0 to 23, 24 to 47, ...) at most 7 rows name the same one
- w_gate: bfloat16 [8, 3072, 8192], P('exp', None, 'ten'), may hold values from -0.109375 to 0.109375
- w_up: bfloat16 [8, 3072, 8192], P('exp', None, 'ten'), may hold values from -0.109375 to 0.109375
- w_down: bfloat16 [8, 8192, 3072], P('exp', 'ten'), may hold values from -0.0625 to 0.0625
Outputs:
- layer_out: bfloat16 [768, 3072], P(('rep', 'exp', 'ten')), parts along dimension 0
There are 2 independent parts, one for each index of `rep`. A program takes and returns all parts, laid end to end along the dimension named above; an argument that names none is the same for every part. Nothing has to cross between parts.
Inputs may be any that keep to these rules, and one draw needn't show every extreme that they name: `expert_ids`: each row names two different experts. Within each aligned block of 24 rows (the rows of one device) no expert is named by more than 7 rows, and in some block one expert is named by exactly 7 rows.
All inputs are finite; a program needn't handle non-finite values.
Results may differ from a plain program's by a relative error of at most 0.013.
Values may be sent and summed in bfloat16 or wider, within the bound.
No kernel may reach another device: no remote copies, remote signals or barrier semaphores. Data moves between devices by JAX's collectives and lax.ppermute only.
A program may use at most 128 MiB of HBM per device.

v0:
```python
import jax
import jax.numpy as jnp
from jax import lax
from jax.sharding import PartitionSpec as P

HD = 128
CAP = 7
lowest_score = -1e30


def local_softmax(scores, visible):
    masked = jnp.where(visible, scores, lowest_score)
    row_max = jnp.max(masked, axis=-1)
    exponent = jnp.where(visible, jnp.exp(masked - row_max[..., None]), 0.0)
    return (row_max, exponent, jnp.sum(exponent, axis=-1))


def on_device(
    hidden_in,
    queries,
    new_kv,
    prefix_kv,
    decode_kv,
    prefix_len,
    decode_len,
    out_proj,
    norm_gain,
    router_w,
    expert_ids,
    w_gate,
    w_up,
    w_down,
):
    ten_size = lax.axis_size("ten")
    groups = lax.axis_size("exp")
    my_ten = lax.axis_index("ten")
    rows_dev, model_width = hidden_in.shape
    dec_dev = decode_len.shape[0]
    span_dev = rows_dev - dec_dev
    span_rows = span_dev * ten_size
    kv_width = new_kv.shape[2]
    heads_kv = kv_width // HD
    heads_q = queries.shape[1] // HD
    per_kv = heads_q // heads_kv
    score_scale = HD ** (-0.5)
    ctx_len = decode_kv.shape[2]
    own_heads = queries.reshape(rows_dev, heads_kv, per_kv, HD)
    dec_keys = jnp.concatenate([decode_kv[0], new_kv[0, span_dev:, None]], axis=1).reshape(
        dec_dev, ctx_len + 1, heads_kv, HD
    )
    dec_values = jnp.concatenate([decode_kv[1], new_kv[1, span_dev:, None]], axis=1).reshape(
        dec_dev, ctx_len + 1, heads_kv, HD
    )
    dec_scores = (
        jnp.einsum(
            "dcgh,dpch->dcgp", own_heads[span_dev:], dec_keys, preferred_element_type=jnp.float32
        )
        * score_scale
    )
    dec_pos = jnp.arange(ctx_len + 1, dtype=jnp.int32)[None, :]
    dec_visible = ((dec_pos < decode_len[:, None]) | (dec_pos == ctx_len))[:, None, None, :]
    dec_max, dec_exponent, dec_totals = local_softmax(dec_scores, dec_visible)
    dec_partial = jnp.einsum(
        "dcgp,dpch->dcgh",
        dec_exponent.astype(jnp.bfloat16),
        dec_values,
        preferred_element_type=jnp.float32,
    )
    full_prefix, full_fresh = (
        lax.all_gather(prefix_kv[:, 0], "ten", axis=1, tiled=True),
        lax.all_gather(new_kv[:, :span_dev], "ten", axis=1, tiled=True),
    )
    prefix_total = full_prefix.shape[1]
    key_rows = jnp.concatenate([full_prefix[0], full_fresh[0]], axis=0).reshape(
        prefix_total + span_rows, heads_kv, HD
    )
    value_rows = jnp.concatenate([full_prefix[1], full_fresh[1]], axis=0).reshape(
        prefix_total + span_rows, heads_kv, HD
    )
    scores = (
        jnp.einsum(
            "rcgh,pch->rcgp", own_heads[:span_dev], key_rows, preferred_element_type=jnp.float32
        )
        * score_scale
    )
    query_row = my_ten * span_dev + jnp.arange(span_dev, dtype=jnp.int32)[:, None]
    positions = jnp.arange(prefix_total + span_rows, dtype=jnp.int32)[None, :]
    visible = jnp.where(
        positions < prefix_total, positions < prefix_len[0], positions - prefix_total <= query_row
    )[:, None, None, :]
    row_max, exponent, totals = local_softmax(scores, visible)
    span_out = (
        jnp.einsum(
            "rcgp,pch->rcgh",
            exponent.astype(jnp.bfloat16),
            value_rows,
            preferred_element_type=jnp.float32,
        )
        / totals[..., None]
    )
    dec_out = dec_partial / dec_totals[..., None]
    attended_rows = (
        jnp.concatenate([span_out, dec_out], axis=0)
        .reshape(rows_dev, heads_q * HD)
        .astype(jnp.bfloat16)
    )
    attended = lax.all_to_all(attended_rows, "ten", split_axis=1, concat_axis=0, tiled=True)
    row_block = attended
    projected = lax.psum_scatter(
        jnp.dot(row_block, out_proj, preferred_element_type=jnp.float32).astype(jnp.bfloat16),
        "ten",
        scatter_dimension=0,
        tiled=True,
    ).astype(jnp.float32)
    residual = hidden_in.astype(jnp.float32) + projected
    mean_square = jnp.mean(residual * residual, axis=1, keepdims=True)
    normed = (residual * lax.rsqrt(mean_square + 1e-05) * norm_gain).astype(jnp.bfloat16)
    logits = jnp.dot(normed, router_w, preferred_element_type=jnp.float32)
    experts = router_w.shape[1]
    chosen_hot = (expert_ids[:, :, None] == jnp.arange(experts, dtype=jnp.int32)).astype(jnp.int32)
    chosen_logits = jnp.sum(jnp.where(chosen_hot == 1, logits[:, None, :], 0.0), axis=2)
    route_weights = jax.nn.softmax(chosen_logits, axis=1)
    flat_hot = chosen_hot.reshape(rows_dev * 2, experts)
    slot_rank = jnp.sum((jnp.cumsum(flat_hot, axis=0) - flat_hot) * flat_hot, axis=1).reshape(
        rows_dev, 2
    )
    capacity = CAP
    slot_index = jnp.arange(capacity, dtype=jnp.int32)
    assignment = chosen_hot[:, :, :, None] * (slot_rank[:, :, None, None] == slot_index).astype(
        jnp.int32
    )
    placement = jnp.sum(assignment, axis=1)
    local_experts = experts // groups
    placement_split = placement.reshape(rows_dev, groups, local_experts, capacity).astype(
        jnp.bfloat16
    )
    outgoing = jnp.einsum(
        "rnlc,rd->lncd", placement_split, normed, preferred_element_type=jnp.float32
    ).astype(jnp.bfloat16)
    arrived = lax.all_to_all(outgoing, "exp", split_axis=1, concat_axis=1, tiled=True)
    shard_rows = lax.all_gather(arrived, "ten", axis=1, tiled=True)
    gate_act = jnp.einsum("lscd,ldf->lscf", shard_rows, w_gate, preferred_element_type=jnp.float32)
    up_act = jnp.einsum("lscd,ldf->lscf", shard_rows, w_up, preferred_element_type=jnp.float32)
    hidden = (jax.nn.silu(gate_act) * up_act).astype(jnp.bfloat16)
    row_block = hidden
    summed = lax.psum_scatter(
        jnp.einsum("lscf,lfd->slcd", row_block, w_down, preferred_element_type=jnp.float32).astype(
            jnp.bfloat16
        ),
        "ten",
        scatter_dimension=0,
        tiled=True,
    )
    returned = lax.all_to_all(summed, "exp", split_axis=0, concat_axis=0, tiled=True)
    outputs = returned.reshape(experts * capacity, model_width).astype(jnp.float32)
    weight_map = jnp.sum(
        assignment.astype(jnp.float32) * route_weights[:, :, None, None], axis=1
    ).reshape(rows_dev, experts * capacity)
    expert_mix = jnp.dot(
        weight_map, outputs, precision=lax.Precision.HIGHEST, preferred_element_type=jnp.float32
    )
    return (residual + expert_mix).astype(jnp.bfloat16)


def solution(mesh):
    in_specs = (
        P(("rep", "exp", "ten"), None),
        P(("rep", "exp", "ten"), None),
        P(None, ("rep", "exp", "ten"), None),
        P(None, ("rep", "exp"), "ten", None),
        P(None, ("rep", "exp", "ten"), None, None),
        P(("rep", "exp")),
        P(("rep", "exp", "ten")),
        P("ten", None),
        P(),
        P(),
        P(("rep", "exp", "ten"), None),
        P("exp", None, "ten"),
        P("exp", None, "ten"),
        P("exp", "ten", None),
    )
    out_specs = P(("rep", "exp", "ten"), None)
    return jax.shard_map(
        on_device, mesh=mesh, in_specs=in_specs, out_specs=out_specs, check_vma=False
    )
```

profile of v0, /device:TPU:0, one launch (start us, length us, event | category | flops | bytes accessed | tf_op | source)
XLA Modules:
  0.0 201.0 jit_solution(10028590843201728159)
XLA Ops:
  6.6 0.8 fusion.119
  7.3 1.2 fusion.117
  9.4 0.5 fusion.120
  10.1 7.6 %all_gather.10 = bf16[2,80,1024]{2,0,1:T(2,128)(2,1)S(1)} all-gather(bf16[2,20,1024]{2,0,1:T(2,128)(2,1)S(1)} %copy.122), channel_id=1, replica_groups=mesh['rep'=2,'exp'=4,'ten'=4] {'ten'}, dimensions={1}, use_global_device_ids=true | all-gather | bytes 409600 | tf_op jit(solution)/shard_map/all_gather | solution.py:71
  17.7 1.4 slice_reduce_fusion
  19.3 7.3 %all-gather = bf16[2,1,128,1024]{3,0,1,2:T(2,128)(2,1)S(1)} all-gather(bf16[2,1,32,1024]{3,0,1,2:T(2,128)(2,1)S(1)} %copy.87), channel_id=2, replica_groups=mesh['rep'=2,'exp'=4,'ten'=4] {'ten'}, dimensions={2}, use_global_device_ids=true | all-gather | bytes 655360 | tf_op jit(solution)/shard_map/all_gather | solution.py:70
  26.6 0.7 fusion.118
  27.3 0.4 copy.121
  28.6 0.4 copy.123
  29.6 0.5 fusion.49
  30.4 0.7 fusion.123
  31.2 0.8 fusion.35
  32.3 8.8 %all_to_all.26 = bf16[24,4,1536]{2,0,1:T(8,128)(2,1)S(1)} all-to-all(bf16[24,4,1536]{2,0,1:T(8,128)(2,1)S(1)} %copy.103), channel_id=1, replica_groups=mesh['rep'=2,'exp'=4,'ten'=4] {'ten'}, dimensions={1} | all-to-all | bytes 589824 | tf_op jit(solution)/shard_map/all_to_all | solution.py:107
  41.1 6.2 %convolution_convert_fusion = bf16[96,3072]{1,0:T(8,128)(2,1)} fusion(bf16[96,1536]{1,0:T(8,128)(2,1)S(1)} %bitcast.127, bf16[1536,3072]{1,0:T(8,128)(2,1)} %param.21), kind=kOutput, calls=%fused_computation.10 | convolution fusion | flops 906264576 | bytes 10321920 | tf_op jit(solution)/shard_map/dot_general | solution.py:110
  48.2 0.6 copy-done.7
  48.8 0.6 copy-done.9
  49.4 20.6 %reduce-scatter.3.cloned.1.call-done = bf16[24,3072]{1,0:T(8,128)(2,1)} async-done(((bf16[96,3072]{1,0:T(8,128)(2,1)}), bf16[24,3072]{1,0:T(8,128)(2,1)}) %reduce-scatter.3.cloned.1.call-update) | async-done | bytes 147472 | tf_op jit(solution)/shard_map/reduce_scatter | solution.py:109
  70.0 1.1 multiply_reduce_fusion
  71.0 1.0 multiply_convert_fusion
  72.3 0.4 copy.108
  72.7 14.9 %all_to_all.27 = bf16[2,4,7,3072]{3,0,2,1:T(2,128)(2,1)} all-to-all(bf16[2,4,7,3072]{3,0,2,1:T(2,128)(2,1)S(1)} %copy.108), channel_id=1, replica_groups=mesh['rep'=2,'exp'=4,'ten'=4] {'exp'}, dimensions={1} | all-to-all | bytes 688128 | tf_op jit(solution)/shard_map/all_to_all | solution.py:140
  87.9 16.6 %all-gather.3.cloned.1.call-done = bf16[2,16,7,3072]{3,0,2,1:T(2,128)(2,1)} async-done(((bf16[2,4,7,3072]{3,0,2,1:T(2,128)(2,1)}), bf16[2,16,7,3072]{3,0,2,1:T(2,128)(2,1)}) %all-gather.3.cloned.1.call-update) | async-done | bytes 1376272 | tf_op jit(solution)/shard_map/all_gather | solution.py:141
  104.5 10.9 %fusion.6 = f32[2,16,7,2048]{3,1,2,0:T(8,128)S(1)} fusion(bf16[2,3072,2048]{2,1,0:T(8,128)(2,1)} %param.25, bf16[2,16,7,3072]{3,0,2,1:T(2,128)(2,1)} %all-gather.3.cloned.1.call-done), kind=kOutput, calls=%fused_computation.6 | convolution fusion | flops 2818572288 | bytes 28377088 | tf_op jit(solution)/shard_map/lscd,ldf->lscf/dot_general | solution.py:142
  115.4 20.2 %fusion.11 = bf16[16,2,7,3072]{3,0,2,1:T(8,128)(2,1)} fusion(bf16[2,2048,3072]{2,1,0:T(8,128)(2,1)} %param.27, bf16[2,3072,2048]{2,1,0:T(8,128)(2,1)} %param.26, f32[2,16,7,2048]{3,1,2,0:T(8,128)S(1)} %fusion.6, bf16[2,16,7,3072]{3,0,2,1:T(2,128)(2,1)S(1)} %copy-done.1), kind=kOutput, calls=%fused_computation.9 | convolution fusion | flops 5640585216 | bytes 54919168 | tf_op jit(solution)/shard_map/lscf,lfd->slcd/dot_general | solution.py:147
  135.7 0.6 copy-done.15
  136.3 0.6 dynamic-slice
  137.7 38.1 %all-reduce.3.cloned.1.call-done = bf16[16,2,7,3072]{3,0,2,1:T(8,128)(2,1)} async-done(((bf16[16,2,7,3072]{3,0,2,1:T(8,128)(2,1)}), bf16[16,2,7,3072]{3,0,2,1:T(8,128)(2,1)}) %all-reduce.3.cloned.1.call-update) | async-done | bytes 1376272
  175.9 1.3 constant_dynamic-slice_fusion
  177.1 1.0 copy.111
  178.1 4.6 %all-to-all-start.2 = ((bf16[4,2,7,3072]{3,1,2,0:T(2,128)(2,1)}), bf16[4,2,7,3072]{3,1,2,0:T(2,128)(2,1)S(1)}, u32[]{:S(2)}, u32[]{:S(2)}) async-start(bf16[4,2,7,3072]{3,1,2,0:T(2,128)(2,1)} %copy.111), calls=%async_computation.3 | async-start | bytes 688128 | tf_op jit(solution)/shard_map/all_to_all | solution.py:154
  182.9 10.4 %all-to-all-done.2 = bf16[4,2,7,3072]{3,1,2,0:T(2,128)(2,1)S(1)} async-done(((bf16[4,2,7,3072]{3,1,2,0:T(2,128)(2,1)}), bf16[4,2,7,3072]{3,1,2,0:T(2,128)(2,1)S(1)}, u32[]{:S(2)}, u32[]{:S(2)}) %all-to-all-start.2) | async-done | bytes 344096 | tf_op jit(solution)/shard_map/all_to_all | solution.py:154
  193.5 1.0 fusion.15
  (84 shorter events, 4.3 us)
Async XLA Ops:
  6.5 131.0 %copy-start = (bf16[3072,8]{0,1:T(8,128)(2,1)S(1)}, bf16[3072,8]{0,1:T(8,128)(2,1)}, u32[]{:S(2)}) copy-start(bf16[3072,8]{0,1:T(8,128)(2,1)} %param.23) | copy-start | bytes 147460
  6.5 63.4 %reduce-scatter.3.cloned.1.call-start = ((), (), s32[]{:S(2)}) async-start(), calls=%async_computation.4 | async-start | bytes 737280 | tf_op jit(solution)/shard_map/reduce_scatter | solution.py:109
  7.3 1.4 copy-start.4
  8.6 0.7 copy-start.14
  8.9 1.2 copy-start.5
  9.4 9.8 %copy-start.6 = (bf16[2,1,32,1024]{3,2,1,0:T(8,128)(2,1)S(1)}, bf16[2,1,32,1024]{3,2,1,0:T(8,128)(2,1)}, u32[]{:S(2)}) copy-start(bf16[2,1,32,1024]{3,2,1,0:T(8,128)(2,1)} %param.17) | copy-start | bytes 393220
  41.1 6.3 %copy-start.12 = (s32[24,2]{0,1:T(2,128)S(1)}, s32[24,2]{0,1:T(2,128)}, u32[]{:S(2)}) copy-start(s32[24,2]{0,1:T(2,128)} %param.24) | copy-start | bytes 580
  41.1 28.8 %copy-start.2 = (bf16[24,3072]{1,0:T(8,128)(2,1)S(1)}, bf16[24,3072]{1,0:T(8,128)(2,1)}, u32[]{:S(2)}) copy-start(bf16[24,3072]{1,0:T(8,128)(2,1)} %param.14) | copy-start | bytes 442372
  41.1 29.9 %copy-start.11 = (f32[3072]{0:T(1024)S(1)}, f32[3072]{0:T(1024)}, u32[]{:S(2)}) copy-start(f32[3072]{0:T(1024)} %param.22) | copy-start | bytes 36868
  47.4 57.1 %all-gather.3.cloned.1.call-start = ((), (), s32[]{:S(2)}) async-start(), calls=%async_computation.5 | async-start | bytes 1720320 | tf_op jit(solution)/shard_map/all_gather | solution.py:141
  48.2 0.6 copy-start.7
  48.8 0.6 copy-start.9
  87.7 88.2 %all-reduce.3.cloned.1.call-start = ((), (), s32[]{:S(2)}) async-start(), calls=%async_computation.6 | async-start | bytes 2752512
  104.5 10.9 %copy-start.1 = (bf16[2,16,7,3072]{3,0,2,1:T(2,128)(2,1)S(1)}, bf16[2,16,7,3072]{3,0,2,1:T(2,128)(2,1)}, u32[]{:S(2)}) copy-start(bf16[2,16,7,3072]{3,0,2,1:T(2,128)(2,1)} %all-gather.3.cloned.1.call-done) | copy-start | bytes 4128772
  135.6 0.7 copy-start.15
  135.7 47.1 %copy-start.13 = (s32[24,2]{0,1:T(2,128)S(1)}, s32[24,2]{0,1:T(2,128)}, u32[]{:S(2)}) copy-start(s32[24,2]{0,1:T(2,128)} %param.24) | copy-start | bytes 580
  135.7 47.1 %copy-start.8 = (s32[24,2,8]{0,2,1:T(8,128)S(1)}, s32[24,2,8]{0,2,1:T(8,128)}, u32[]{:S(2)}) copy-start(s32[24,2,8]{0,2,1:T(8,128)} %copy-done.7) | copy-start | bytes 4612
  135.7 47.1 %copy-start.10 = (s32[24,2,7]{0,2,1:T(8,128)S(1)}, s32[24,2,7]{0,2,1:T(8,128)}, u32[]{:S(2)}) copy-start(s32[24,2,7]{0,2,1:T(8,128)} %copy-done.9) | copy-start | bytes 4036
  177.1 16.3 %copy-start.3 = (bf16[24,3072]{1,0:T(8,128)(2,1)S(1)}, bf16[24,3072]{1,0:T(8,128)(2,1)}, u32[]{:S(2)}) copy-start(bf16[24,3072]{1,0:T(8,128)(2,1)} %reduce-scatter.3.cloned.1.call-done) | copy-start | bytes 442372
  178.1 15.1 %all-to-all-start.2 = ((bf16[4,2,7,3072]{3,1,2,0:T(2,128)(2,1)}), bf16[4,2,7,3072]{3,1,2,0:T(2,128)(2,1)S(1)}, u32[]{:S(2)}, u32[]{:S(2)}) async-start(bf16[4,2,7,3072]{3,1,2,0:T(2,128)(2,1)} %copy.111), calls=%async_computation.3 | async-start | bytes 688128 | tf_op jit(solution)/shard_map/all_to_all | solution.py:154
Sparse Core Ops, SparseCore 0:
  47.5 22.3 reduce-scatter.2
  87.8 16.6 all-gather.2
  135.8 40.0 all-reduce.2
where the time goes:
time: 201 us
  waiting for transfers between devices  85.7 us (43%)
  matrix products  41.3 us (21%)
  blocking collectives  38.6 us (19%)
  between operations  14.8 us (7%)
  local copies, waits for them, and re-layouts  12.7 us (6%)
  starting transfers between devices  4.87 us (2%)
  other arithmetic  2.9 us (1%)
    unnamed x4, waiting for transfers between devices  38.2 us
    reduce_scatter x1, waiting for transfers between devices, on_device(): lax.psum_scatter(jnp.dot(row_block, out_proj, preferred_element_type=jnp....  20.6 us
    dot_general x1, matrix products, on_device(): jnp.einsum('lscf,lfd->slcd', row_block, w_down, preferred_element_type=jn...  20.2 us
    all_gather x1, waiting for transfers between devices, on_device(): shard_rows = lax.all_gather(arrived, 'ten', axis=1, tiled=True)  16.6 us
    all_to_all x1, blocking collectives, on_device(): lax.all_to_all(outgoing, 'exp', split_axis=1, concat_axis=1, tiled=True)  14.9 us
    dot_general x1, matrix products, on_device(): jnp.einsum('lscd,ldf->lscf', shard_rows, w_gate, preferred_element_type=j...  10.9 us
    all_to_all x1, waiting for transfers between devices, on_device(): lax.all_to_all(summed, 'exp', split_axis=0, concat_axis=0, tiled=True)  10.4 us
    all_to_all x1, blocking collectives, on_device(): lax.all_to_all(attended_rows, 'ten', split_axis=1, concat_axis=0, tiled=T...  8.78 us
  transfers between devices with their start and end apart: 4, of which 4 were waited for; matrix products, arithmetic and copies ran while one was open for 1% of the time, Pallas kernels for 0%

commit v1 on v0

--- a/solution.py
+++ b/solution.py
@@ -137,7 +137,15 @@
     outgoing = jnp.einsum(
         "rnlc,rd->lncd", placement_split, normed, preferred_element_type=jnp.float32
     ).astype(jnp.bfloat16)
-    arrived = lax.all_to_all(outgoing, "exp", split_axis=1, concat_axis=1, tiled=True)
+    ways, here = (lax.axis_size("exp"), lax.axis_index("exp"))
+    width = outgoing.shape[1] // ways
+    turned = jnp.roll(outgoing, -here * width, axis=1)
+    got = [lax.slice_in_dim(turned, 0, width, axis=1)]
+    for far in range(1, ways):
+        sent = lax.slice_in_dim(turned, far * width, (far + 1) * width, axis=1)
+        got.append(lax.ppermute(sent, "exp", [(d, (d + far) % ways) for d in range(ways)]))
+    line = jnp.concatenate(got[::-1], axis=1)
+    arrived = jnp.roll(line, (here + 1) * got[0].shape[1], axis=1)
     shard_rows = lax.all_gather(arrived, "ten", axis=1, tiled=True)
     gate_act = jnp.einsum("lscd,ldf->lscf", shard_rows, w_gate, preferred_element_type=jnp.float32)
     up_act = jnp.einsum("lscd,ldf->lscf", shard_rows, w_up, preferred_element_type=jnp.float32)

time: 201 us -> 201 us (level)
  blocking collectives: 38.6 us -> 23.7 us
  waiting for transfers between devices: 85.7 us -> 94 us
  starting transfers between devices: 4.87 us -> 9.33 us
    all_to_all x1 -> x0, blocking collectives: 14.9 us -> none  [on_device(): lax.all_to_all(outgoing, 'exp', split_axis=1, concat_axis=1, tiled=True)]
    ppermute x0 -> x3, waiting for transfers between devices: none -> 7.47 us  [on_device(): lax.ppermute(sent, 'exp', [(d, (d + far) % ways) for d in range(ways)])]
    ppermute x0 -> x3, starting transfers between devices: none -> 4.47 us  [on_device(): lax.ppermute(sent, 'exp', [(d, (d + far) % ways) for d in range(ways)])]
  transfers between devices with their start and end apart: 4 -> 7, of which waited for: 4 -> 6; matrix products, arithmetic and copies ran while one was open for 1% -> 1% of each run, Pallas kernels for 0% -> 0%
where the time goes in v1:
time: 201 us; the launch traced here: 200 us
  waiting for transfers between devices  94 us (47%)
  matrix products  41.3 us (21%)
  blocking collectives  23.7 us (12%)
  between operations  14.9 us (7%)
  local copies, waits for them, and re-layouts  13.5 us (7%)
  starting transfers between devices  9.33 us (5%)
  other arithmetic  3.73 us (2%)
    unnamed x4, waiting for transfers between devices  38.1 us
    reduce_scatter x1, waiting for transfers between devices, on_device(): lax.psum_scatter(jnp.dot(row_block, out_proj, preferred_element_type=jnp....  20.6 us
    dot_general x1, matrix products, on_device(): jnp.einsum('lscf,lfd->slcd', row_block, w_down, preferred_element_type=jn...  20.2 us
    all_gather x1, waiting for transfers between devices, on_device(): shard_rows = lax.all_gather(arrived, 'ten', axis=1, tiled=True)  17.5 us
    dot_general x1, matrix products, on_device(): jnp.einsum('lscd,ldf->lscf', shard_rows, w_gate, preferred_element_type=j...  10.9 us
    all_to_all x1, waiting for transfers between devices, on_device(): lax.all_to_all(summed, 'exp', split_axis=0, concat_axis=0, tiled=True)  10.4 us
    all_to_all x1, blocking collectives, on_device(): lax.all_to_all(attended_rows, 'ten', split_axis=1, concat_axis=0, tiled=T...  8.78 us
    all_gather x1, blocking collectives, on_device(): lax.all_gather(new_kv[:, :span_dev], 'ten', axis=1, tiled=True)  7.61 us
  transfers between devices with their start and end apart: 7, of which 6 were waited for; matrix products, arithmetic and copies ran while one was open for 1% of the time, Pallas kernels for 0%

profile of v1, /device:TPU:0, one launch (start us, length us, event | category | flops | bytes accessed | tf_op | source)
XLA Modules:
  0.0 200.5 jit_solution(1567316359936356368)
XLA Ops:
  6.6 0.8 fusion.128
  7.3 1.2 fusion.125
  10.1 7.6 %all_gather.10 = bf16[2,80,1024]{2,0,1:T(2,128)(2,1)S(1)} all-gather(bf16[2,20,1024]{2,0,1:T(2,128)(2,1)S(1)} %copy.122), channel_id=1, replica_groups=mesh['rep'=2,'exp'=4,'ten'=4] {'ten'}, dimensions={1}, use_global_device_ids=true | all-gather | bytes 409600 | tf_op jit(solution)/shard_map/all_gather | solution.py:71
  17.7 1.4 slice_reduce_fusion
  19.3 7.3 %all-gather = bf16[2,1,128,1024]{3,0,1,2:T(2,128)(2,1)S(1)} all-gather(bf16[2,1,32,1024]{3,0,1,2:T(2,128)(2,1)S(1)} %copy.87), channel_id=2, replica_groups=mesh['rep'=2,'exp'=4,'ten'=4] {'ten'}, dimensions={2}, use_global_device_ids=true | all-gather | bytes 655360 | tf_op jit(solution)/shard_map/all_gather | solution.py:70
  26.6 0.7 fusion.126
  30.4 0.7 fusion.132
  31.2 0.8 fusion.35
  32.3 8.8 %all_to_all.21 = bf16[24,4,1536]{2,0,1:T(8,128)(2,1)S(1)} all-to-all(bf16[24,4,1536]{2,0,1:T(8,128)(2,1)S(1)} %copy.103), channel_id=1, replica_groups=mesh['rep'=2,'exp'=4,'ten'=4] {'ten'}, dimensions={1} | all-to-all | bytes 589824 | tf_op jit(solution)/shard_map/all_to_all | solution.py:107
  41.1 6.2 %convolution_convert_fusion = bf16[96,3072]{1,0:T(8,128)(2,1)} fusion(bf16[96,1536]{1,0:T(8,128)(2,1)S(1)} %bitcast.127, bf16[1536,3072]{1,0:T(8,128)(2,1)} %param.23), kind=kOutput, calls=%fused_computation.10 | convolution fusion | flops 906264576 | bytes 10321920 | tf_op jit(solution)/shard_map/dot_general | solution.py:110
  48.2 0.6 copy-done.7
  48.8 0.6 copy-done.9
  49.4 20.6 %reduce-scatter.3.cloned.1.call-done = bf16[24,3072]{1,0:T(8,128)(2,1)} async-done(((bf16[96,3072]{1,0:T(8,128)(2,1)}), bf16[24,3072]{1,0:T(8,128)(2,1)}) %reduce-scatter.3.cloned.1.call-update) | async-done | bytes 147472 | tf_op jit(solution)/shard_map/reduce_scatter | solution.py:109
  70.0 1.1 multiply_reduce_fusion
  71.0 1.0 multiply_convert_fusion
  72.6 3.4 %collective-permute-start = (bf16[2,1,7,3072]{3,2,0,1:T(8,128)(2,1)S(1)}, bf16[2,1,7,3072]{3,2,0,1:T(8,128)(2,1)S(1)}, u32[]{:S(2)}, u32[]{:S(2)}) collective-permute-start(bf16[2,1,7,3072]{3,2,0,1:T(8,128)(2,1)S(1)} %get-tuple-element.15), channel_id=1, source_target_pairs={{0,12},{4,0},{8,4},{12,8},{1,13},{5,1},{9,5},{13,9},{2,14},{6,2},{... | collective-permute-start | bytes 258056 | tf_op jit(solution)/shard_map/ppermute | solution.py:146
  75.9 1.1 collective-permute-start.2
  77.0 2.1 %collective-permute-done = bf16[2,1,7,3072]{3,2,0,1:T(8,128)(2,1)S(1)} collective-permute-done((bf16[2,1,7,3072]{3,2,0,1:T(8,128)(2,1)S(1)}, bf16[2,1,7,3072]{3,2,0,1:T(8,128)(2,1)S(1)}, u32[]{:S(2)}, u32[]{:S(2)}) %collective-permute-start) | collective-permute-done | bytes 86048 | tf_op jit(solution)/shard_map/ppermute | solution.py:146
  79.1 5.4 %collective-permute-done.1 = bf16[2,1,7,3072]{3,2,0,1:T(8,128)(2,1)S(1)} collective-permute-done((bf16[2,1,7,3072]{3,2,0,1:T(8,128)(2,1)S(1)}, bf16[2,1,7,3072]{3,2,0,1:T(8,128)(2,1)S(1)}, u32[]{:S(2)}, u32[]{:S(2)}) %collective-permute-start.1) | collective-permute-done | bytes 86048 | tf_op jit(solution)/shard_map/ppermute | solution.py:146
  84.5 0.6 fusion.60
  85.1 1.1 copy.108
  86.5 17.5 %all-gather.3.cloned.1.call-done = bf16[2,16,7,3072]{3,0,2,1:T(2,128)(2,1)} async-done(((bf16[2,4,7,3072]{3,0,2,1:T(2,128)(2,1)}), bf16[2,16,7,3072]{3,0,2,1:T(2,128)(2,1)}) %all-gather.3.cloned.1.call-update) | async-done | bytes 1376272 | tf_op jit(solution)/shard_map/all_gather | solution.py:149
  104.0 10.9 %fusion.6 = f32[2,16,7,2048]{3,1,2,0:T(8,128)S(1)} fusion(bf16[2,3072,2048]{2,1,0:T(8,128)(2,1)} %param.27, bf16[2,16,7,3072]{3,0,2,1:T(2,128)(2,1)} %all-gather.3.cloned.1.call-done), kind=kOutput, calls=%fused_computation.6 | convolution fusion | flops 2818572288 | bytes 28377088 | tf_op jit(solution)/shard_map/lscd,ldf->lscf/dot_general | solution.py:150
  114.9 20.2 %fusion.11 = bf16[16,2,7,3072]{3,0,2,1:T(8,128)(2,1)} fusion(bf16[2,2048,3072]{2,1,0:T(8,128)(2,1)} %param.29, bf16[2,3072,2048]{2,1,0:T(8,128)(2,1)} %param.28, f32[2,16,7,2048]{3,1,2,0:T(8,128)S(1)} %fusion.6, bf16[2,16,7,3072]{3,0,2,1:T(2,128)(2,1)S(1)} %copy-done.1), kind=kOutput, calls=%fused_computation.9 | convolution fusion | flops 5640585216 | bytes 54919168 | tf_op jit(solution)/shard_map/lscf,lfd->slcd/dot_general | solution.py:155
  135.2 0.6 copy-done.15
  135.8 0.6 dynamic-slice
  137.3 38.1 %all-reduce.3.cloned.1.call-done = bf16[16,2,7,3072]{3,0,2,1:T(8,128)(2,1)} async-done(((bf16[16,2,7,3072]{3,0,2,1:T(8,128)(2,1)}), bf16[16,2,7,3072]{3,0,2,1:T(8,128)(2,1)}) %all-reduce.3.cloned.1.call-update) | async-done | bytes 1376272
  175.3 1.3 constant_dynamic-slice_fusion
  176.6 1.0 copy.111
  177.6 4.6 %all-to-all-start.1 = ((bf16[4,2,7,3072]{3,1,2,0:T(2,128)(2,1)}), bf16[4,2,7,3072]{3,1,2,0:T(2,128)(2,1)S(1)}, u32[]{:S(2)}, u32[]{:S(2)}) async-start(bf16[4,2,7,3072]{3,1,2,0:T(2,128)(2,1)} %copy.111), calls=%async_computation.2 | async-start | bytes 688128 | tf_op jit(solution)/shard_map/all_to_all | solution.py:162
  182.4 10.4 %all-to-all-done.1 = bf16[4,2,7,3072]{3,1,2,0:T(2,128)(2,1)S(1)} async-done(((bf16[4,2,7,3072]{3,1,2,0:T(2,128)(2,1)}), bf16[4,2,7,3072]{3,1,2,0:T(2,128)(2,1)S(1)}, u32[]{:S(2)}, u32[]{:S(2)}) %all-to-all-start.1) | async-done | bytes 344096 | tf_op jit(solution)/shard_map/all_to_all | solution.py:162
  192.9 1.0 fusion.15
  (92 shorter events, 6.4 us)
Async XLA Ops:
  6.5 130.6 %copy-start = (bf16[3072,8]{0,1:T(8,128)(2,1)S(1)}, bf16[3072,8]{0,1:T(8,128)(2,1)}, u32[]{:S(2)}) copy-start(bf16[3072,8]{0,1:T(8,128)(2,1)} %param.25) | copy-start | bytes 147460
  6.5 63.4 %reduce-scatter.3.cloned.1.call-start = ((), (), s32[]{:S(2)}) async-start(), calls=%async_computation.3 | async-start | bytes 737280 | tf_op jit(solution)/shard_map/reduce_scatter | solution.py:109
  7.3 1.4 copy-start.4
  8.6 0.7 copy-start.14
  8.9 1.2 copy-start.5
  9.4 9.8 %copy-start.6 = (bf16[2,1,32,1024]{3,2,1,0:T(8,128)(2,1)S(1)}, bf16[2,1,32,1024]{3,2,1,0:T(8,128)(2,1)}, u32[]{:S(2)}) copy-start(bf16[2,1,32,1024]{3,2,1,0:T(8,128)(2,1)} %param.19) | copy-start | bytes 393220
  41.1 6.4 %copy-start.12 = (s32[24,2]{0,1:T(2,128)S(1)}, s32[24,2]{0,1:T(2,128)}, u32[]{:S(2)}) copy-start(s32[24,2]{0,1:T(2,128)} %param.26) | copy-start | bytes 580
  41.1 28.8 %copy-start.2 = (bf16[24,3072]{1,0:T(8,128)(2,1)S(1)}, bf16[24,3072]{1,0:T(8,128)(2,1)}, u32[]{:S(2)}) copy-start(bf16[24,3072]{1,0:T(8,128)(2,1)} %param.16) | copy-start | bytes 442372
  41.1 29.9 %copy-start.11 = (f32[3072]{0:T(1024)S(1)}, f32[3072]{0:T(1024)}, u32[]{:S(2)}) copy-start(f32[3072]{0:T(1024)} %param.24) | copy-start | bytes 36868
  47.4 56.6 %all-gather.3.cloned.1.call-start = ((), (), s32[]{:S(2)}) async-start(), calls=%async_computation.4 | async-start | bytes 1720320 | tf_op jit(solution)/shard_map/all_gather | solution.py:149
  48.2 0.6 copy-start.7
  48.8 0.6 copy-start.9
  72.6 6.6 %collective-permute-start = (bf16[2,1,7,3072]{3,2,0,1:T(8,128)(2,1)S(1)}, bf16[2,1,7,3072]{3,2,0,1:T(8,128)(2,1)S(1)}, u32[]{:S(2)}, u32[]{:S(2)}) collective-permute-start(bf16[2,1,7,3072]{3,2,0,1:T(8,128)(2,1)S(1)} %get-tuple-element.15), channel_id=1, source_target_pairs={{0,12},{4,0},{8,4},{12,8},{1,13},{5,1},{9,5},{13,9},{2,14},{6,2},{... | collective-permute-start | bytes 258056 | tf_op jit(solution)/shard_map/ppermute | solution.py:146
  75.9 8.6 %collective-permute-start.1 = (bf16[2,1,7,3072]{3,2,0,1:T(8,128)(2,1)S(1)}, bf16[2,1,7,3072]{3,2,0,1:T(8,128)(2,1)S(1)}, u32[]{:S(2)}, u32[]{:S(2)}) collective-permute-start(bf16[2,1,7,3072]{3,2,0,1:T(8,128)(2,1)S(1)} %get-tuple-element.14), channel_id=1, source_target_pairs={{0,8},{4,12},{8,0},{12,4},{1,9},{5,13},{9,1},{13,5},{2,10},{6,14},... | collective-permute-start | bytes 258056 | tf_op jit(solution)/shard_map/ppermute | solution.py:146
  75.9 8.6 %collective-permute-start.2 = (bf16[2,1,7,3072]{3,2,0,1:T(8,128)(2,1)S(1)}, bf16[2,1,7,3072]{3,2,0,1:T(8,128)(2,1)S(1)}, u32[]{:S(2)}, u32[]{:S(2)}) collective-permute-start(bf16[2,1,7,3072]{3,2,0,1:T(8,128)(2,1)S(1)} %get-tuple-element.13), channel_id=1, source_target_pairs={{0,4},{4,8},{8,12},{12,0},{1,5},{5,9},{9,13},{13,1},{2,6},{6,10},{... | collective-permute-start | bytes 258056 | tf_op jit(solution)/shard_map/ppermute | solution.py:146
  86.3 89.1 %all-reduce.3.cloned.1.call-start = ((), (), s32[]{:S(2)}) async-start(), calls=%async_computation.5 | async-start | bytes 2752512
  104.0 10.9 %copy-start.1 = (bf16[2,16,7,3072]{3,0,2,1:T(2,128)(2,1)S(1)}, bf16[2,16,7,3072]{3,0,2,1:T(2,128)(2,1)}, u32[]{:S(2)}) copy-start(bf16[2,16,7,3072]{3,0,2,1:T(2,128)(2,1)} %all-gather.3.cloned.1.call-done) | copy-start | bytes 4128772
  135.2 0.7 copy-start.15
  135.2 47.0 %copy-start.13 = (s32[24,2]{0,1:T(2,128)S(1)}, s32[24,2]{0,1:T(2,128)}, u32[]{:S(2)}) copy-start(s32[24,2]{0,1:T(2,128)} %param.26) | copy-start | bytes 580
  135.2 47.1 %copy-start.8 = (s32[24,2,8]{0,2,1:T(8,128)S(1)}, s32[24,2,8]{0,2,1:T(8,128)}, u32[]{:S(2)}) copy-start(s32[24,2,8]{0,2,1:T(8,128)} %copy-done.7) | copy-start | bytes 4612
  135.2 47.1 %copy-start.10 = (s32[24,2,7]{0,2,1:T(8,128)S(1)}, s32[24,2,7]{0,2,1:T(8,128)}, u32[]{:S(2)}) copy-start(s32[24,2,7]{0,2,1:T(8,128)} %copy-done.9) | copy-start | bytes 4036
  176.6 16.3 %copy-start.3 = (bf16[24,3072]{1,0:T(8,128)(2,1)S(1)}, bf16[24,3072]{1,0:T(8,128)(2,1)}, u32[]{:S(2)}) copy-start(bf16[24,3072]{1,0:T(8,128)(2,1)} %reduce-scatter.3.cloned.1.call-done) | copy-start | bytes 442372
  177.6 15.1 %all-to-all-start.1 = ((bf16[4,2,7,3072]{3,1,2,0:T(2,128)(2,1)}), bf16[4,2,7,3072]{3,1,2,0:T(2,128)(2,1)S(1)}, u32[]{:S(2)}, u32[]{:S(2)}) async-start(bf16[4,2,7,3072]{3,1,2,0:T(2,128)(2,1)} %copy.111), calls=%async_computation.2 | async-start | bytes 688128 | tf_op jit(solution)/shard_map/all_to_all | solution.py:162
Sparse Core Ops, SparseCore 0:
  47.5 22.3 reduce-scatter.2
  86.4 17.5 all-gather.2
  135.3 39.9 all-reduce.2
